TPU v7x, 128 devices: a whole 4x4x4 slice. The times are simulated.
128 devices in a mesh: z: 4 (over z), y: 4 (over y), xc: 8 (over x, core).
Axes of the slice: x: 4, y: 4, z: 4, core: 2. Of those that a mesh axis runs over, the one named last changes fastest.
Arguments:
- tokens_x: bfloat16 [32768, 1536], P(('z', 'y', 'xc'))
- grad_y: bfloat16 [32768, 1536], P(('z', 'y', 'xc'))
- w_one: bfloat16 [1536, 6144], replicated
- w_two: bfloat16 [6144, 1536], replicated
- w_three: bfloat16 [1536, 6144], replicated
- w_four: bfloat16 [6144, 1536], replicated
Outputs:
- output 1: float32 [1536, 6144], replicated
- output 2: float32 [6144, 1536], replicated
- output 3: float32 [1536, 6144], replicated
- output 4: float32 [6144, 1536], replicated
All inputs are finite; a program needn't handle non-finite values.
Results may differ from a plain program's by a relative error of at most 0.00433.
Values are sent between devices in bfloat16 or wider.
A program may use at most 1 GiB of HBM per device.

v0:
```python
import math
import jax
import jax.numpy as jnp
from jax import lax
from jax.sharding import PartitionSpec as P

GELU_SCALE = math.sqrt(2.0 / math.pi)
GELU_CUBIC = 0.044715


def gelu_value(pre_act):
    return 0.5 * pre_act * (1.0 + jnp.tanh(GELU_SCALE * (pre_act + GELU_CUBIC * pre_act * pre_act * pre_act)))


def gelu_grad(pre_act):
    tanh_val = jnp.tanh(GELU_SCALE * (pre_act + GELU_CUBIC * pre_act * pre_act * pre_act))
    return 0.5 * (1.0 + tanh_val) + 0.5 * pre_act * (1.0 - tanh_val * tanh_val) * GELU_SCALE * (1.0 + 3.0 * GELU_CUBIC * pre_act * pre_act)


def solution(mesh):
    n_dev = math.prod(mesh.shape.values())
    batch_spec = P(("z", "y", "xc"), None)
    whole_spec = P(None, None)

    def reduce_grad(local_grad):
        reduced = lax.psum_scatter(local_grad, "xc", scatter_dimension=0, tiled=True)
        reduced = lax.psum_scatter(reduced, "y", scatter_dimension=0, tiled=True)
        reduced = lax.psum(reduced, "z")
        reduced = lax.all_gather(reduced, "y", axis=0, tiled=True)
        reduced = lax.all_gather(reduced, "xc", axis=0, tiled=True)
        return reduced / n_dev

    def device_step(x_loc, g_loc, w_one, w_two, w_three, w_four):
        a_one = jnp.dot(x_loc, w_one, preferred_element_type=jnp.float32).astype(jnp.bfloat16)
        h_one = gelu_value(a_one.astype(jnp.float32)).astype(jnp.bfloat16)
        h_two = (jnp.dot(h_one, w_two, preferred_element_type=jnp.float32) + x_loc.astype(jnp.float32)).astype(jnp.bfloat16)
        a_three = jnp.dot(h_two, w_three, preferred_element_type=jnp.float32).astype(jnp.bfloat16)
        h_three = gelu_value(a_three.astype(jnp.float32)).astype(jnp.bfloat16)
        grad_w4 = reduce_grad(jnp.einsum("nf,nd->fd", h_three, g_loc, preferred_element_type=jnp.float32))
        d_a3 = (jnp.einsum("nd,fd->nf", g_loc, w_four, preferred_element_type=jnp.float32) * gelu_grad(a_three.astype(jnp.float32))).astype(jnp.bfloat16)
        grad_w3 = reduce_grad(jnp.einsum("nd,nf->df", h_two, d_a3, preferred_element_type=jnp.float32))
        d_h2 = (jnp.einsum("nf,df->nd", d_a3, w_three, preferred_element_type=jnp.float32) + g_loc.astype(jnp.float32)).astype(jnp.bfloat16)
        grad_w2 = reduce_grad(jnp.einsum("nf,nd->fd", h_one, d_h2, preferred_element_type=jnp.float32))
        d_a1 = (jnp.einsum("nd,fd->nf", d_h2, w_two, preferred_element_type=jnp.float32) * gelu_grad(a_one.astype(jnp.float32))).astype(jnp.bfloat16)
        grad_w1 = reduce_grad(jnp.einsum("nd,nf->df", x_loc, d_a1, preferred_element_type=jnp.float32))
        return grad_w1, grad_w2, grad_w3, grad_w4

    return jax.shard_map(
        device_step,
        mesh=mesh,
        in_specs=(batch_spec, batch_spec, whole_spec, whole_spec, whole_spec, whole_spec),
        out_specs=(whole_spec, whole_spec, whole_spec, whole_spec),
        check_vma=False,
    )
```

profile of v0, /device:TPU:1, one launch (start us, length us, event | category | flops | bytes accessed | tf_op | source)
XLA Modules:
  0.0 2183.8 jit_solution(12669015822460002356)
XLA Ops:
  7.2 9.4 convolution_convert_fusion.1
  19.3 5.8 fusion.28
  25.1 11.7 convolution_convert_fusion
  36.8 13.4 fusion
  50.3 17.6 fusion.42
  68.0 11.0 fusion.29
  79.0 23.4 %convolution_bitcast_fusion = f32[1536,6144]{0,1:T(8,128)} fusion(bf16[256,1536]{1,0:T(8,128)(2,1)} %param.6, bf16[256,1536]{1,0:T(8,128)(2,1)} %fusion.29, bf16[6144,1536]{1,0:T(8,128)(2,1)} %param.9, bf16[256,6144]{1,0:T(8,128)(2,1)S(1)} %convolution_convert_fusion.1), kind=kOutput, calls=%fused_computation | convolution fusion | flops 9695133696 | bytes 61341696 | tf_op jit(solution)/shard_map/nd,nf->df/dot_general | solution.py:45
  102.4 36.8 %copy.17 = f32[1536,6144]{1,0:T(8,128)} copy(f32[1536,6144]{0,1:T(8,128)} %convolution_bitcast_fusion) | data formatting | bytes 75497472
  139.3 18.0 fusion.20
  157.4 17.7 fusion.39
  175.1 85.8 %reduce-scatter.29.cloned.1.call-done = f32[192,6144]{1,0:T(8,128)} async-done(((f32[1536,6144]{1,0:T(8,128)}), f32[192,6144]{1,0:T(8,128)}) %reduce-scatter.29.cloned.1.call-update) | async-done | bytes 4718608
  261.0 192.9 %reduce-scatter.25.cloned.1.call-done = f32[192,6144]{1,0:T(8,128)} async-done(((f32[1536,6144]{1,0:T(8,128)}), f32[192,6144]{1,0:T(8,128)}) %reduce-scatter.25.cloned.1.call-update) | async-done | bytes 4718608
  454.0 192.9 %reduce-scatter.21.cloned.1.call-done = f32[768,1536]{1,0:T(8,128)} async-done(((f32[6144,1536]{1,0:T(8,128)}), f32[768,1536]{1,0:T(8,128)}) %reduce-scatter.21.cloned.1.call-update) | async-done | bytes 4718608 | tf_op jit(solution)/shard_map/reduce_scatter | solution.py:26
  646.9 192.7 %reduce-scatter.17.cloned.1.call-done = f32[768,1536]{1,0:T(8,128)} async-done(((f32[6144,1536]{1,0:T(8,128)}), f32[768,1536]{1,0:T(8,128)}) %reduce-scatter.17.cloned.1.call-update) | async-done | bytes 4718608 | tf_op jit(solution)/shard_map/reduce_scatter | solution.py:26
  839.7 53.3 %reduce-scatter.31.cloned.1.call-done = f32[48,6144]{1,0:T(8,128)} async-done(((f32[192,6144]{1,0:T(8,128)}), f32[48,6144]{1,0:T(8,128)}) %reduce-scatter.31.cloned.1.call-update) | async-done | bytes 1179664
  896.2 50.0 %reduce-scatter.27.cloned.1.call-done = f32[48,6144]{1,0:T(8,128)} async-done(((f32[192,6144]{1,0:T(8,128)}), f32[48,6144]{1,0:T(8,128)}) %reduce-scatter.27.cloned.1.call-update) | async-done | bytes 1179664
  949.4 50.1 %reduce-scatter.23.cloned.1.call-done = f32[192,1536]{1,0:T(8,128)} async-done(((f32[768,1536]{1,0:T(8,128)}), f32[192,1536]{1,0:T(8,128)}) %reduce-scatter.23.cloned.1.call-update) | async-done | bytes 1179664 | tf_op jit(solution)/shard_map/reduce_scatter | solution.py:27
  999.5 53.3 %reduce-scatter.19.cloned.1.call-done = f32[192,1536]{1,0:T(8,128)} async-done(((f32[768,1536]{1,0:T(8,128)}), f32[192,1536]{1,0:T(8,128)}) %reduce-scatter.19.cloned.1.call-update) | async-done | bytes 1179664 | tf_op jit(solution)/shard_map/reduce_scatter | solution.py:27
  1052.9 167.7 %all-reduce.3.cloned.1.call-done = (f32[48,6144]{0,1:T(8,128)}, f32[192,1536]{1,0:T(8,128)}, f32[48,6144]{0,1:T(8,128)}, f32[192,1536]{1,0:T(8,128)}) async-done(((f32[48,6144]{0,1:T(8,128)}, f32[192,1536]{1,0:T(8,128)}, f32[48,6144]{0,1:T(8,128)}, f32[192,1536]{1,0:T(8,128)}), (f32[48,6144]{0,1:T(8,128)}, f32[192,1536]{1,0:T(8,128)}, f32[48,6144]{0,1:T(8,128)}, ...) | async-done | bytes 4718608 | tf_op jit(solution)/shard_map/psum | solution.py:28
  1220.5 3.3 copy.13
  1227.2 48.9 %all-gather.9.cloned.1.call-done = f32[192,6144]{1,0:T(8,128)} async-done(((f32[48,6144]{1,0:T(8,128)}), f32[192,6144]{1,0:T(8,128)}) %all-gather.9.cloned.1.call-update) | async-done | bytes 4718608 | tf_op jit(solution)/shard_map/all_gather | solution.py:29
  1276.2 54.6 %all-gather.13.cloned.1.call-done = f32[768,1536]{1,0:T(8,128)} async-done(((f32[192,1536]{1,0:T(8,128)}), f32[768,1536]{1,0:T(8,128)}) %all-gather.13.cloned.1.call-update) | async-done | bytes 4718608 | tf_op jit(solution)/shard_map/all_gather | solution.py:29
  1330.9 54.4 %all-gather.21.cloned.1.call-done = f32[768,1536]{1,0:T(8,128)} async-done(((f32[192,1536]{1,0:T(8,128)}), f32[768,1536]{1,0:T(8,128)}) %all-gather.21.cloned.1.call-update) | async-done | bytes 4718608 | tf_op jit(solution)/shard_map/all_gather | solution.py:29
  1385.3 55.1 %all-gather.17.cloned.1.call-done = f32[192,6144]{1,0:T(8,128)} async-done(((f32[48,6144]{1,0:T(8,128)}), f32[192,6144]{1,0:T(8,128)}) %all-gather.17.cloned.1.call-update) | async-done | bytes 4718608 | tf_op jit(solution)/shard_map/all_gather | solution.py:29
  1440.5 178.7 %all-gather.11.cloned.1.call-done = f32[1536,6144]{1,0:T(8,128)} async-done(((f32[192,6144]{1,0:T(8,128)}), f32[1536,6144]{1,0:T(8,128)}) %all-gather.11.cloned.1.call-update) | async-done | bytes 37748752 | tf_op jit(solution)/shard_map/all_gather | solution.py:30
  1619.2 27.8 %broadcast_multiply_fusion.3 = f32[1536,6144]{1,0:T(8,128)} fusion(f32[1536,6144]{1,0:T(8,128)} %all-gather.11.cloned.1.call-done), kind=kLoop, calls=%fused_computation.4 | loop fusion | flops 9437184 | bytes 75497472 | tf_op jit(solution)/shard_map/div | solution.py:31
  1647.0 148.9 %all-gather.15.cloned.1.call-done = f32[6144,1536]{1,0:T(8,128)} async-done(((f32[768,1536]{1,0:T(8,128)}), f32[6144,1536]{1,0:T(8,128)}) %all-gather.15.cloned.1.call-update) | async-done | bytes 37748752 | tf_op jit(solution)/shard_map/all_gather | solution.py:30
  1795.9 27.7 %broadcast_multiply_fusion.1 = f32[6144,1536]{1,0:T(8,128)} fusion(f32[6144,1536]{1,0:T(8,128)} %all-gather.15.cloned.1.call-done), kind=kLoop, calls=%fused_computation.2 | loop fusion | flops 9437184 | bytes 75497472 | tf_op jit(solution)/shard_map/div | solution.py:31
  1823.7 149.0 %all-gather.23.cloned.1.call-done = f32[6144,1536]{1,0:T(8,128)} async-done(((f32[768,1536]{1,0:T(8,128)}), f32[6144,1536]{1,0:T(8,128)}) %all-gather.23.cloned.1.call-update) | async-done | bytes 37748752 | tf_op jit(solution)/shard_map/all_gather | solution.py:30
  1972.7 27.7 %broadcast_multiply_fusion = f32[6144,1536]{1,0:T(8,128)} fusion(f32[6144,1536]{1,0:T(8,128)} %all-gather.23.cloned.1.call-done), kind=kLoop, calls=%fused_computation.1 | loop fusion | flops 9437184 | bytes 75497472 | tf_op jit(solution)/shard_map/div | solution.py:31
  2000.4 149.0 %all-gather.19.cloned.1.call-done = f32[1536,6144]{1,0:T(8,128)} async-done(((f32[192,6144]{1,0:T(8,128)}), f32[1536,6144]{1,0:T(8,128)}) %all-gather.19.cloned.1.call-update) | async-done | bytes 37748752 | tf_op jit(solution)/shard_map/all_gather | solution.py:30
  2149.4 27.8 %broadcast_multiply_fusion.2 = f32[1536,6144]{1,0:T(8,128)} fusion(f32[1536,6144]{1,0:T(8,128)} %all-gather.19.cloned.1.call-done), kind=kLoop, calls=%fused_computation.3 | loop fusion | flops 9437184 | bytes 75497472 | tf_op jit(solution)/shard_map/div | solution.py:31
  (47 shorter events, 13.2 us)
Async XLA Ops:
  7.2 253.8 %reduce-scatter.29.cloned.1.call-start = ((), (), s32[]{:S(2)}) async-start(), calls=%async_computation.22 | async-start | bytes 42467328
  7.2 12.0 copy-start.3
  7.2 12.1 copy-start.4
  25.1 11.7 copy-start.2
  36.8 13.5 copy-start
  67.9 386.0 %reduce-scatter.25.cloned.1.call-start = ((), (), s32[]{:S(2)}) async-start(), calls=%async_computation.20 | async-start | bytes 42467328
  139.2 507.6 %reduce-scatter.21.cloned.1.call-start = ((), (), s32[]{:S(2)}) async-start(), calls=%async_computation.16 | async-start | bytes 42467328 | tf_op jit(solution)/shard_map/reduce_scatter | solution.py:26
  157.3 682.3 %reduce-scatter.17.cloned.1.call-start = ((), (), s32[]{:S(2)}) async-start(), calls=%async_computation.10 | async-start | bytes 42467328 | tf_op jit(solution)/shard_map/reduce_scatter | solution.py:26
  175.1 718.0 %reduce-scatter.31.cloned.1.call-start = ((), (), s32[]{:S(2)}) async-start(), calls=%async_computation.23 | async-start | bytes 5898240
  261.0 685.2 %reduce-scatter.27.cloned.1.call-start = ((), (), s32[]{:S(2)}) async-start(), calls=%async_computation.21 | async-start | bytes 5898240
  453.9 545.6 %reduce-scatter.23.cloned.1.call-start = ((), (), s32[]{:S(2)}) async-start(), calls=%async_computation.17 | async-start | bytes 5898240 | tf_op jit(solution)/shard_map/reduce_scatter | solution.py:27
  646.9 405.9 %reduce-scatter.19.cloned.1.call-start = ((), (), s32[]{:S(2)}) async-start(), calls=%async_computation.11 | async-start | bytes 5898240 | tf_op jit(solution)/shard_map/reduce_scatter | solution.py:27
  839.7 380.8 %all-reduce.3.cloned.1.call-start = ((), (), s32[]{:S(2)}) async-start(), calls=%async_computation.24 | async-start | bytes 17301504 | tf_op jit(solution)/shard_map/psum | solution.py:28
  1052.8 223.3 %all-gather.9.cloned.1.call-start = ((), (), s32[]{:S(2)}) async-start(), calls=%async_computation.8 | async-start | bytes 5898240 | tf_op jit(solution)/shard_map/all_gather | solution.py:29
  1220.5 4.7 copy-start.1
  1223.8 107.0 %all-gather.13.cloned.1.call-start = ((), (), s32[]{:S(2)}) async-start(), calls=%async_computation.12 | async-start | bytes 5898240 | tf_op jit(solution)/shard_map/all_gather | solution.py:29
  1224.6 160.7 %all-gather.21.cloned.1.call-start = ((), (), s32[]{:S(2)}) async-start(), calls=%async_computation.18 | async-start | bytes 5898240 | tf_op jit(solution)/shard_map/all_gather | solution.py:29
  1225.2 215.3 %all-gather.17.cloned.1.call-start = ((), (), s32[]{:S(2)}) async-start(), calls=%async_computation.14 | async-start | bytes 5898240 | tf_op jit(solution)/shard_map/all_gather | solution.py:29
  1227.2 392.0 %all-gather.11.cloned.1.call-start = ((), (), s32[]{:S(2)}) async-start(), calls=%async_computation.9 | async-start | bytes 42467328 | tf_op jit(solution)/shard_map/all_gather | solution.py:30
  1276.2 519.7 %all-gather.15.cloned.1.call-start = ((), (), s32[]{:S(2)}) async-start(), calls=%async_computation.13 | async-start | bytes 42467328 | tf_op jit(solution)/shard_map/all_gather | solution.py:30
  1330.8 641.8 %all-gather.23.cloned.1.call-start = ((), (), s32[]{:S(2)}) async-start(), calls=%async_computation.19 | async-start | bytes 42467328 | tf_op jit(solution)/shard_map/all_gather | solution.py:30
  1385.3 764.1 %all-gather.19.cloned.1.call-start = ((), (), s32[]{:S(2)}) async-start(), calls=%async_computation.15 | async-start | bytes 42467328 | tf_op jit(solution)/shard_map/all_gather | solution.py:30
Sparse Core Ops, SparseCore 0:
  68.0 192.8 reduce-scatter.28
  264.0 189.8 reduce-scatter.24
  457.0 189.8 reduce-scatter.20
  649.8 189.8 reduce-scatter.16
  841.9 51.0 reduce-scatter.30
  895.3 50.8 reduce-scatter.26
  948.6 50.8 reduce-scatter.22
  1001.9 50.8 reduce-scatter.18
  1056.2 164.2 all-reduce.2
  1224.0 52.1 all-gather.8
  1277.8 52.9 all-gather.12
  1332.3 52.9 all-gather.20
  1387.5 52.9 all-gather.16
  1442.0 177.1 all-gather.10
  1620.7 175.1 all-gather.14
  1797.5 175.1 all-gather.22
  1974.2 175.1 all-gather.18
where the time goes:
time: 2190 us; the launch traced here: 2180 us
  waiting for transfers between devices  1880 us (86%)
  matrix products  128 us (6%)
  other arithmetic  111 us (5%)
  local copies, waits for them, and re-layouts  51.1 us (2%)
    all_gather x4, waiting for transfers between devices, reduce_grad(): reduced = lax.all_gather(reduced, 'xc', axis=0, tiled=True)  626 us
    reduce_scatter x2, waiting for transfers between devices, reduce_grad(): lax.psum_scatter(local_grad, 'xc', scatter_dimension=0, tiled=True)  386 us
    unnamed x21, waiting for transfers between devices  383 us
    all_gather x4, waiting for transfers between devices, reduce_grad(): reduced = lax.all_gather(reduced, 'y', axis=0, tiled=True)  213 us
    psum x1, waiting for transfers between devices, reduce_grad(): reduced = lax.psum(reduced, 'z')  168 us
    div x4, other arithmetic, reduce_grad(): return reduced / n_dev  111 us
    reduce_scatter x2, waiting for transfers between devices, reduce_grad(): reduced = lax.psum_scatter(reduced, 'y', scatter_dimension=0, tiled=True)  103 us
    unnamed x13, local copies, waits for them, and re-layouts  45.9 us
  transfers between devices with their start and end apart: 17, of which 17 were waited for; matrix products, arithmetic and copies ran while one was open for 9% of the time, Pallas kernels for 0%

commit v1 on v0

v1 whole, which is shorter than its diff:
```python
import functools
import math
import jax
import jax.numpy as jnp
from jax import lax
from jax.experimental import pallas as pl
from jax.experimental.pallas import tpu as pltpu
from jax.sharding import PartitionSpec as P

GELU_SCALE = math.sqrt(2.0 / math.pi)
GELU_CUBIC = 0.044715


def gelu_value(pre_act):
    return 0.5 * pre_act * (1.0 + jnp.tanh(GELU_SCALE * (pre_act + GELU_CUBIC * pre_act * pre_act * pre_act)))


def gelu_grad(pre_act):
    tanh_val = jnp.tanh(GELU_SCALE * (pre_act + GELU_CUBIC * pre_act * pre_act * pre_act))
    return 0.5 * (1.0 + tanh_val) + 0.5 * pre_act * (1.0 - tanh_val * tanh_val) * GELU_SCALE * (1.0 + 3.0 * GELU_CUBIC * pre_act * pre_act)


def place_kernel(moves, depth, *refs):
    n_src = len({m[0] for m in moves})
    srcs, dsts = refs[:n_src], refs[n_src:-3]
    slots, in_sem, out_sem = refs[-3:]

    def load(step):
        src, src_row, _, _, rows = moves[step]
        return pltpu.make_async_copy(srcs[src].at[pl.ds(src_row, rows)], slots.at[step % depth], in_sem.at[step % depth])

    def store(step):
        _, _, dst, dst_row, rows = moves[step]
        return pltpu.make_async_copy(slots.at[step % depth], dsts[dst].at[pl.ds(dst_row, rows)], out_sem.at[step % depth])

    ahead = depth // 2
    for step in range(min(ahead, len(moves))):
        load(step).start()
    for step in range(len(moves)):
        if step + ahead < len(moves):
            if step + ahead >= depth:
                store(step + ahead - depth).wait()
            load(step + ahead).start()
        load(step).wait()
        store(step).start()
    for step in range(max(0, len(moves) - depth), len(moves)):
        store(step).wait()


def place(src, n_dst, rows):
    total, width = src.shape
    out_rows = total // n_dst
    moves = [(0, row, row // out_rows, row % out_rows, rows) for row in range(0, total, rows)]
    depth = 6
    return pl.pallas_call(
        functools.partial(place_kernel, moves, depth),
        out_shape=[jax.ShapeDtypeStruct((out_rows, width), src.dtype)] * n_dst,
        in_specs=[pl.BlockSpec(memory_space=pl.ANY)],
        out_specs=[pl.BlockSpec(memory_space=pl.ANY)] * n_dst,
        scratch_shapes=[pltpu.VMEM((depth, rows, width), src.dtype), pltpu.SemaphoreType.DMA((depth,)), pltpu.SemaphoreType.DMA((depth,))],
        cost_estimate=pl.CostEstimate(flops=8 * src.size, bytes_accessed=8 * src.size, transcendentals=0),
    )(src)


def solution(mesh):
    n_dev = math.prod(mesh.shape.values())
    batch_spec = P(("z", "y", "xc"), None)
    whole_spec = P(None, None)

    axes = ("z", "y", "xc")

    def scatter_sum(local_grad):
        return lax.psum_scatter(local_grad, axes, scatter_dimension=0, tiled=True) * (1.0 / n_dev)

    def gather(part):
        return lax.all_gather(part, axes, axis=0, tiled=True)

    def device_step(x_loc, g_loc, w_one, w_two, w_three, w_four):
        a_one = jnp.dot(x_loc, w_one, preferred_element_type=jnp.float32).astype(jnp.bfloat16)
        h_one = gelu_value(a_one.astype(jnp.float32)).astype(jnp.bfloat16)
        h_two = (jnp.dot(h_one, w_two, preferred_element_type=jnp.float32) + x_loc.astype(jnp.float32)).astype(jnp.bfloat16)
        a_three = jnp.dot(h_two, w_three, preferred_element_type=jnp.float32).astype(jnp.bfloat16)
        h_three = gelu_value(a_three.astype(jnp.float32)).astype(jnp.bfloat16)
        part_w4 = scatter_sum(jnp.einsum("nf,nd->fd", h_three, g_loc, preferred_element_type=jnp.float32))
        d_a3 = (jnp.einsum("nd,fd->nf", g_loc, w_four, preferred_element_type=jnp.float32) * gelu_grad(a_three.astype(jnp.float32))).astype(jnp.bfloat16)
        local_w3 = jnp.einsum("nd,nf->df", h_two, d_a3, preferred_element_type=jnp.float32)
        d_h2 = (jnp.einsum("nf,df->nd", d_a3, w_three, preferred_element_type=jnp.float32) + g_loc.astype(jnp.float32)).astype(jnp.bfloat16)
        local_w2 = jnp.einsum("nf,nd->fd", h_one, d_h2, preferred_element_type=jnp.float32)
        d_a1 = (jnp.einsum("nd,fd->nf", d_h2, w_two, preferred_element_type=jnp.float32) * gelu_grad(a_one.astype(jnp.float32))).astype(jnp.bfloat16)
        local_w1 = jnp.einsum("nd,nf->df", x_loc, d_a1, preferred_element_type=jnp.float32)
        part_w4, local_w2 = lax.optimization_barrier((part_w4, local_w2))
        part_w2 = scatter_sum(local_w2)
        part_w2, local_w13 = lax.optimization_barrier((part_w2, jnp.concatenate([local_w1, local_w3], axis=0)))
        part_w13 = scatter_sum(local_w13)
        grad_w13 = gather(part_w13)
        part_w4, grad_w13 = lax.optimization_barrier((part_w4, grad_w13))
        grad_w4 = gather(part_w4)
        part_w2, grad_w4 = lax.optimization_barrier((part_w2, grad_w4))
        grad_w2 = gather(part_w2)
        grad_w1, grad_w3 = place(grad_w13, 2, 96)
        (grad_w4,) = place(grad_w4, 1, 384)
        (grad_w2,) = place(grad_w2, 1, 384)
        return grad_w1, grad_w2, grad_w3, grad_w4

    return jax.shard_map(
        device_step,
        mesh=mesh,
        in_specs=(batch_spec, batch_spec, whole_spec, whole_spec, whole_spec, whole_spec),
        out_specs=(whole_spec, whole_spec, whole_spec, whole_spec),
        check_vma=False,
    )
```

time: 2190 us -> 1450 us (0.66)
  waiting for transfers between devices: 1880 us -> 1150 us
  Pallas kernels: 0 us -> 100 us
  other arithmetic: 111 us -> 54.3 us
  local copies, waits for them, and re-layouts: 51.1 us -> 2.58 us
    all_gather x8 -> x3, waiting for transfers between devices: 839 us -> 335 us  [gather(): return lax.all_gather(part, axes, axis=0, tiled=True)]
    psum x1 -> x0, waiting for transfers between devices: 168 us -> none  [reduce_grad(): reduced = lax.psum(reduced, 'z')]
    div x4 -> x0, other arithmetic: 111 us -> none  [reduce_grad(): return reduced / n_dev]
    pallas_call x0 -> x3, Pallas kernels: none -> 100 us  [place(): pl.pallas_call(functools.partial(place_kernel, moves, depth), out_shape=[...]
    reduce_scatter x4 -> x2, waiting for transfers between devices: 489 us -> 433 us  [scatter_sum(): lax.psum_scatter(local_grad, axes, scatter_dimension=0, tiled=True)]
    concatenate x0 -> x1, other arithmetic: none -> 49 us  [device_step(): jnp.concatenate([local_w1, local_w3], axis=0)]
    unnamed x13 -> x14, local copies, waits for them, and re-layouts: 45.9 us -> 2.58 us
    unnamed x21 -> x7, waiting for transfers between devices: 383 us -> 384 us
  transfers between devices with their start and end apart: 17 -> 6, of which waited for: 17 -> 6; matrix products, arithmetic and copies ran while one was open for 9% -> 9% of each run, Pallas kernels for 0% -> 5%
where the time goes in v1:
time: 1450 us
  waiting for transfers between devices  1150 us (79%)
  matrix products  127 us (9%)
  Pallas kernels  100 us (7%)
  other arithmetic  54.3 us (4%)
    reduce_scatter x2, waiting for transfers between devices, scatter_sum(): lax.psum_scatter(local_grad, axes, scatter_dimension=0, tiled=True)  433 us
    unnamed x7, waiting for transfers between devices  384 us
    all_gather x3, waiting for transfers between devices, gather(): return lax.all_gather(part, axes, axis=0, tiled=True)  335 us
    pallas_call x3, Pallas kernels, place(): pl.pallas_call(functools.partial(place_kernel, moves, depth), out_shape=[...  100 us
    concatenate x1, other arithmetic, device_step(): jnp.concatenate([local_w1, local_w3], axis=0)  49 us
  transfers between devices with their start and end apart: 6, of which 6 were waited for; matrix products, arithmetic and copies ran while one was open for 9% of the time, Pallas kernels for 5%

profile of v1, /device:TPU:1, one launch (start us, length us, event | category | flops | bytes accessed | tf_op | source)
XLA Modules:
  0.0 1450.7 jit_solution(2700584308549539846)
XLA Ops:
  7.2 0.0 reduce-scatter.6.cloned.1.call-start
  7.2 9.3 convolution_convert_fusion.1
  16.5 9.7 fusion.26
  26.3 11.9 convolution_convert_fusion
  38.2 1.7 copy-done
  39.9 16.3 %fusion.20 = f32[6144,1536]{1,0:T(8,128)} fusion(bf16[256,1536]{1,0:T(8,128)(2,1)S(1)} %copy-done.3, bf16[256,6144]{1,0:T(8,128)(2,1)S(1)} %convolution_convert_fusion), kind=kOutput, calls=%fused_computation.40 | convolution fusion | flops 4847566848 | bytes 41680896 | tf_op jit(solution)/shard_map/nf,nd->fd/dot_general | solution.py:84
  56.2 0.0 reduce-scatter.6.cloned.1.call-update
  56.2 0.2 reduce-scatter.8.cloned.1.call-start
  56.4 11.9 fusion
  68.4 10.3 fusion.27
  78.7 0.9 copy-done.5
  79.6 16.3 %fusion.37 = f32[6144,1536]{1,0:T(8,128)} fusion(bf16[256,1536]{1,0:T(8,128)(2,1)S(1)} %fusion.27, bf16[256,6144]{1,0:T(8,128)(2,1)S(1)} %convolution_convert_fusion.1), kind=kOutput, calls=%fused_computation.61 | convolution fusion | flops 4847566848 | bytes 41680896 | tf_op jit(solution)/shard_map/nf,nd->fd/dot_general | solution.py:88
  95.9 241.4 %reduce-scatter.6.cloned.1.call-done = f32[48,1536]{1,0:T(8,128)} async-done(((f32[6144,1536]{1,0:T(8,128)}), f32[48,1536]{1,0:T(8,128)}) %reduce-scatter.6.cloned.1.call-update) | async-done | bytes 294928 | tf_op jit(solution)/shard_map/reduce_scatter | solution.py:73
  337.3 1.7 broadcast_multiply_fusion.2
  339.0 0.0 reduce-scatter.8.cloned.1.call-update
  339.0 0.3 reduce-scatter.10.cloned.1.call-start
  339.3 17.3 %fusion.40 = f32[1536,6144]{1,0:T(8,128)} fusion(bf16[256,1536]{1,0:T(8,128)(2,1)} %copy-done.2, bf16[256,6144]{1,0:T(8,128)(2,1)} %copy-done.1), kind=kOutput, calls=%fused_computation.62 | convolution fusion | flops 4831838208 | bytes 41680896 | tf_op jit(solution)/shard_map/nd,nf->df/dot_general | solution.py:86
  356.6 23.6 %convolution_bitcast_fusion = f32[1536,6144]{1,0:T(8,128)} fusion(bf16[256,1536]{1,0:T(8,128)(2,1)} %param.6, bf16[256,1536]{1,0:T(8,128)(2,1)} %copy-done.5, bf16[6144,1536]{1,0:T(8,128)(2,1)} %param.9, bf16[256,6144]{1,0:T(8,128)(2,1)S(1)} %convolution_convert_fusion.1), kind=kOutput, calls=%fused_computation.1 | convolution fusion | flops 9695133696 | bytes 61341696 | tf_op jit(solution)/shard_map/nd,nf->df/dot_general | solution.py:90
  380.2 49.0 %pad_maximum_fusion = f32[3072,6144]{1,0:T(8,128)} fusion(f32[1536,6144]{1,0:T(8,128)} %fusion.40, f32[1536,6144]{1,0:T(8,128)} %convolution_bitcast_fusion), kind=kLoop, calls=%fused_computation | loop fusion | flops 18874368 | bytes 150994944 | tf_op jit(solution)/shard_map/concatenate | solution.py:93
  429.2 191.1 %reduce-scatter.8.cloned.1.call-done = f32[48,1536]{1,0:T(8,128)} async-done(((f32[6144,1536]{1,0:T(8,128)}), f32[48,1536]{1,0:T(8,128)}) %reduce-scatter.8.cloned.1.call-update) | async-done | bytes 294928 | tf_op jit(solution)/shard_map/reduce_scatter | solution.py:73
  620.3 1.7 broadcast_multiply_fusion.1
  622.0 0.0 all-gather.4.cloned.1.call-start
  622.1 384.3 %reduce-scatter.10.cloned.1.call-done = f32[24,6144]{1,0:T(8,128)} async-done(((f32[3072,6144]{1,0:T(8,128)}), f32[24,6144]{1,0:T(8,128)}) %reduce-scatter.10.cloned.1.call-update) | async-done | bytes 589840
  1006.4 1.9 broadcast_multiply_fusion
  1008.3 0.0 all-gather.6.cloned.1.call-start
  1008.3 180.5 %all-gather.4.cloned.1.call-done.refs_0_ = f32[3072,6144]{1,0:T(8,128)} async-done(((f32[24,6144]{1,0:T(8,128)}), f32[3072,6144]{1,0:T(8,128)}) %all-gather.4.cloned.1.call-update) | async-done | bytes 75497488 | tf_op jit(solution)/shard_map/all_gather | solution.py:76
  1188.9 0.0 all-gather.8.cloned.1.call-start
  1188.9 114.3 %all-gather.6.cloned.1.call-done.refs_0_ = f32[6144,1536]{1,0:T(8,128)} async-done(((f32[48,1536]{1,0:T(8,128)}), f32[6144,1536]{1,0:T(8,128)}) %all-gather.6.cloned.1.call-update) | async-done | bytes 37748752 | tf_op jit(solution)/shard_map/all_gather | solution.py:76
  1303.2 49.2 %shard_map.93 = (f32[1536,6144]{1,0:T(8,128)}, f32[1536,6144]{1,0:T(8,128)}) custom-call(f32[3072,6144]{1,0:T(8,128)} %all-gather.4.cloned.1.call-done.refs_0_), custom_call_target="tpu_custom_call" | custom-call | flops 150994944 | bytes 150994944 | tf_op jit(solution)/shard_map/pallas_call | solution.py:55
  1352.4 25.8 %shard_map.95 = f32[6144,1536]{1,0:T(8,128)} custom-call(f32[6144,1536]{1,0:T(8,128)} %all-gather.6.cloned.1.call-done.refs_0_), custom_call_target="tpu_custom_call" | custom-call | flops 75497472 | bytes 75497472 | tf_op jit(solution)/shard_map/pallas_call | solution.py:55
  1378.2 40.2 %all-gather.8.cloned.1.call-done.refs_0_ = f32[6144,1536]{1,0:T(8,128)} async-done(((f32[48,1536]{1,0:T(8,128)}), f32[6144,1536]{1,0:T(8,128)}) %all-gather.8.cloned.1.call-update) | async-done | bytes 37748752 | tf_op jit(solution)/shard_map/all_gather | solution.py:76
  1418.4 25.5 %shard_map.94 = f32[6144,1536]{1,0:T(8,128)} custom-call(f32[6144,1536]{1,0:T(8,128)} %all-gather.8.cloned.1.call-done.refs_0_), custom_call_target="tpu_custom_call" | custom-call | flops 75497472 | bytes 75497472 | tf_op jit(solution)/shard_map/pallas_call | solution.py:55
  (16 shorter events, 0.1 us)
Async XLA Ops:
  7.2 330.1 %reduce-scatter.6.cloned.1.call-start = ((), (), s32[]{:S(2)}) async-start(), calls=%async_computation.3 | async-start | bytes 38043648 | tf_op jit(solution)/shard_map/reduce_scatter | solution.py:73
  7.2 9.3 copy-start.6
  26.2 12.0 copy-start.2
  26.3 13.6 copy-start.3
  38.2 1.7 copy-start
  56.2 564.1 %reduce-scatter.8.cloned.1.call-start = ((), (), s32[]{:S(2)}) async-start(), calls=%async_computation.4 | async-start | bytes 38043648 | tf_op jit(solution)/shard_map/reduce_scatter | solution.py:73
  56.4 11.9 copy-start.4
  68.3 10.3 copy-start.1
  78.7 0.9 copy-start.5
  339.0 667.4 %reduce-scatter.10.cloned.1.call-start = ((), (), s32[]{:S(2)}) async-start(), calls=%async_computation.8 | async-start | bytes 76087296
  622.0 566.8 %all-gather.4.cloned.1.call-start = ((), (), s32[]{:S(2)}) async-start(), calls=%async_computation.5 | async-start | bytes 76087296 | tf_op jit(solution)/shard_map/all_gather | solution.py:76
  1008.3 294.9 %all-gather.6.cloned.1.call-start = ((), (), s32[]{:S(2)}) async-start(), calls=%async_computation.6 | async-start | bytes 38043648 | tf_op jit(solution)/shard_map/all_gather | solution.py:76
  1188.9 229.5 %all-gather.8.cloned.1.call-start = ((), (), s32[]{:S(2)}) async-start(), calls=%async_computation.7 | async-start | bytes 38043648 | tf_op jit(solution)/shard_map/all_gather | solution.py:76
Sparse Core Ops, SparseCore 0:
  56.3 280.9 reduce-scatter.5
  343.3 276.9 reduce-scatter.7
  626.1 380.2 reduce-scatter.9
  1009.8 179.0 all-gather.3
  1191.7 111.4 all-gather.5
  1306.7 111.7 all-gather.7

commit v2 on v0

v2 whole, which is shorter than its diff:
```python
import functools
import math
import jax
import jax.numpy as jnp
from jax import lax
from jax.experimental import pallas as pl
from jax.experimental.pallas import tpu as pltpu
from jax.sharding import PartitionSpec as P

GELU_SCALE = math.sqrt(2.0 / math.pi)
GELU_CUBIC = 0.044715
MESH = pl.DeviceIdType.MESH
RING = 4
PARTS = 3
CHUNKS = 4
BLOCKS = 3
PIECES = 3
LAST = 1


def gelu_value(pre_act):
    return 0.5 * pre_act * (1.0 + jnp.tanh(GELU_SCALE * (pre_act + GELU_CUBIC * pre_act * pre_act * pre_act)))


def gelu_grad(pre_act):
    tanh_val = jnp.tanh(GELU_SCALE * (pre_act + GELU_CUBIC * pre_act * pre_act * pre_act))
    return 0.5 * (1.0 + tanh_val) + 0.5 * pre_act * (1.0 - tanh_val * tanh_val) * GELU_SCALE * (1.0 + 3.0 * GELU_CUBIC * pre_act * pre_act)


def pick(index, values):
    chosen = values[-1]
    for k in range(len(values) - 2, -1, -1):
        chosen = jnp.where(index == k, values[k], chosen)
    return chosen


def reduce_kernel(rows, bm, scale, *refs):
    bn = 2 * bm
    hid, wid = refs[0:4], refs[4:8]
    out_refs = refs[8:10]
    relay_wid, relay_hid = refs[10:12]
    hid_v, wid_v, acc, stage, ring1, ring2, result = refs[12:19]
    (own_sem, near_send, near_recv, hop_send, hop_recv, fwd_send, fwd_recv,
     stage_send, stage_recv, r1_send, r1_recv, r2_send, r2_recv, out_sem) = refs[19:]
    n_stage = stage.shape[0]
    half_rows = rows // 2

    z, y, xc = lax.axis_index("z"), lax.axis_index("y"), lax.axis_index("xc")
    x, core = lax.div(xc, 2), lax.rem(xc, 2)
    coord = (x, y, z)
    partner = (z, y, x * 2 + (1 - core))

    def shifted(axis, direction):
        to = lax.rem(coord[axis] + (1 if direction == 0 else RING - 1), RING)
        return ((z, y, to * 2 + core), (z, to, xc), (to, y, xc))[axis]

    barrier = pltpu.get_barrier_semaphore()
    for axis in range(3):
        for direction in range(2):
            pl.semaphore_signal(barrier, inc=1, device_id=shifted(axis, direction), device_id_type=MESH)
    pl.semaphore_signal(barrier, inc=1, device_id=partner, device_id_type=MESH)
    pl.semaphore_wait(barrier, 7)

    def source(piece, part, which, row, n):
        if piece == 0:
            return wid[which].at[pl.ds(row, n)]
        side = 1 - core if piece == 1 else core
        return hid[which].at[pl.ds(row, n), pl.ds(pl.multiple_of((8 * part + 4 * side) * bm, 4 * bm), 4 * bm)]

    def landing(piece, part, slot, row, n):
        if piece == 0:
            return wid_v.at[part, pl.ds(slot * rows + row, n)]
        return hid_v.at[piece - 1, part, pl.ds(slot * rows + row, n)]

    def relay(piece, part, direction):
        if piece == 0:
            return relay_wid.at[part, direction]
        return relay_hid.at[piece - 1, part, direction]

    def own(piece, part, which):
        return pltpu.make_async_copy(source(piece, part, which, 0, rows), landing(piece, part, 0, 0, rows), own_sem.at[piece, part])

    def near(piece, part, direction, which):
        return pltpu.make_async_remote_copy(
            src_ref=source(piece, part, which, 0, rows), dst_ref=landing(piece, part, 1 + 2 * direction, 0, rows),
            send_sem=near_send.at[piece, part, direction], recv_sem=near_recv.at[piece, part, direction],
            device_id=shifted(part, direction), device_id_type=MESH)

    def hop(piece, part, direction, which):
        return pltpu.make_async_remote_copy(
            src_ref=source(piece, part, which, direction * half_rows, half_rows), dst_ref=relay(piece, part, direction),
            send_sem=hop_send.at[piece, part, direction], recv_sem=hop_recv.at[piece, part, direction],
            device_id=shifted(part, direction), device_id_type=MESH)

    def forward(piece, part, direction):
        return pltpu.make_async_remote_copy(
            src_ref=relay(piece, part, direction), dst_ref=landing(piece, part, 2, direction * half_rows, half_rows),
            send_sem=fwd_send.at[piece, part, direction], recv_sem=fwd_recv.at[piece, part, direction],
            device_id=shifted(part, direction), device_id_type=MESH)

    def start_for(copy, owner):
        for which in range(4):
            @pl.when(owner == which)
            def _():
                copy(which).start()

    def start_hops(piece):
        for part in range(PARTS):
            for direction in range(2):
                start_for(functools.partial(hop, piece, part, direction), lax.rem(coord[part] + 2, RING))

    def start_nears(piece):
        for part in range(PARTS):
            for direction in range(2):
                start_for(functools.partial(near, piece, part, direction), lax.rem(coord[part] + (1 if direction == 0 else 3), RING))

    def pass_on(piece):
        for part in range(PARTS):
            for direction in range(2):
                hop(piece, part, direction, 0).wait_recv()
                forward(piece, part, direction).start()

    def arrived(piece, part):
        own(piece, part, 0).wait()
        for direction in range(2):
            near(piece, part, direction, 0).wait_recv()
            forward(piece, part, direction).wait_recv()

    start_hops(0)
    start_hops(1)
    for piece in range(PIECES):
        for part in range(PARTS):
            start_for(functools.partial(own, piece, part), coord[part])
    start_nears(0)
    start_nears(1)
    pass_on(0)
    pass_on(1)
    start_hops(2)
    start_nears(2)

    def product(side, part, chunk, block, store):
        odd = lax.rem(pick(part, coord), 2)
        dims = (((0,), (0,)), ((), ()))

        @pl.when(odd == 1)
        def _():
            left = hid_v[side, part, :, pl.ds(pl.multiple_of(chunk * bm, bm), bm)]
            right = wid_v[part, :, pl.ds(pl.multiple_of(block * bn, bn), bn)]
            store(lax.dot_general(left, right, dims, preferred_element_type=jnp.float32))

        @pl.when(odd == 0)
        def _():
            index = 3 * chunk + block
            left = wid_v[part, :, pl.ds(pl.multiple_of(lax.div(index, 2) * bm, bm), bm)]
            right = hid_v[side, part, :, pl.ds(pl.multiple_of(lax.rem(index, 2) * bn, bn), bn)]
            store(lax.dot_general(left, right, dims, preferred_element_type=jnp.float32))

    def hand_over(part, chunk, block, slot):
        return pltpu.make_async_remote_copy(
            src_ref=stage.at[slot], dst_ref=acc.at[part, chunk, block], send_sem=stage_send.at[slot],
            recv_sem=stage_recv.at[part, chunk, block], device_id=partner, device_id_type=MESH)

    for part in range(PARTS):
        arrived(0, part)
        arrived(1, part)

        def other_half(step, carry):
            chunk, block = lax.div(step, BLOCKS), lax.rem(step, BLOCKS)
            count = part * CHUNKS * BLOCKS + step
            slot = lax.rem(count, n_stage)

            @pl.when(count >= n_stage)
            def _():
                hand_over(0, 0, 0, slot).wait_send()

            def store(value):
                stage[slot] = value

            product(0, part, chunk, block, store)
            hand_over(part, chunk, block, slot).start()
            return carry

        lax.fori_loop(0, CHUNKS * BLOCKS, other_half, 0)
        if part == 0:
            pass_on(2)

    first = (y, z, x)
    second = (z, x, y)
    top, low = bm // 2, bm // 8

    def ring1_copy(part, direction, step, block):
        chunk = lax.rem(first[part] + (RING - 1 - step if direction == 0 else 1 + step), RING)
        return pltpu.make_async_remote_copy(
            src_ref=acc.at[part, chunk, block, pl.ds(direction * top, top)], dst_ref=ring1.at[part, direction, step, block],
            send_sem=r1_send.at[part, direction, block], recv_sem=r1_recv.at[part, direction, step, block],
            device_id=shifted((part + 1) % 3, direction), device_id_type=MESH)

    for part in range(PARTS):
        arrived(2, part)

    for order, offset in enumerate((3, 1, 2, 0)):

        def own_half(step, carry):
            part, block = lax.div(step, BLOCKS), lax.rem(step, BLOCKS)
            chunk = lax.rem(pick(part, first) + offset, RING)
            hand_over(part, chunk, block, 0).wait_recv()

            def store(value):
                acc[part, chunk, block] = acc[part, chunk, block] + value

            product(1, part, chunk, block, store)
            return carry

        lax.fori_loop(0, PARTS * BLOCKS, own_half, 0)
        if order < 2:
            for block in range(BLOCKS):
                for part in range(PARTS):
                    ring1_copy(part, order, 0, block).start()

    for step in range(RING - 1):
        for block in range(BLOCKS):
            for part in range(PARTS):
                for direction in range(2):
                    ring1_copy(part, direction, step, block).wait_recv()
                    chunk = lax.rem(first[part] + (RING - 2 - step if direction == 0 else 2 + step), RING)
                    share = acc.at[part, chunk, block, pl.ds(direction * top, top)]
                    share[...] = share[...] + ring1[part, direction, step, block]
                    ring1_copy(part, direction, step, block).wait_send()
                    if step < RING - 2:
                        ring1_copy(part, direction, step + 1, block).start()

    def ring2_share(part, direction, place):
        row = pl.multiple_of(2 * low * place + direction * low, low)
        return acc.at[part, first[part], :, pl.ds(row, low)]

    def ring2_copy(part, direction, step):
        place = lax.rem(second[part] + (RING - 1 - step if direction == 0 else 1 + step), RING)
        return pltpu.make_async_remote_copy(
            src_ref=ring2_share(part, direction, place), dst_ref=ring2.at[part, direction, step],
            send_sem=r2_send.at[part, direction], recv_sem=r2_recv.at[part, direction, step],
            device_id=shifted((part + 2) % 3, direction), device_id_type=MESH)

    for part in range(PARTS):
        for direction in range(2):
            ring2_copy(part, direction, 0).start()
    for step in range(RING - 1):
        for part in range(PARTS):
            for direction in range(2):
                ring2_copy(part, direction, step).wait_recv()
                place = lax.rem(second[part] + (RING - 2 - step if direction == 0 else 2 + step), RING)
                share = ring2_share(part, direction, place)
                total = share[...] + ring2[part, direction, step]
                ring2_copy(part, direction, step).wait_send()
                if step < RING - 2:
                    share[...] = total
                    ring2_copy(part, direction, step + 1).start()
                else:
                    result[pl.ds(part * BLOCKS, BLOCKS), pl.ds(direction * low, low)] = total * scale

    n_main = PARTS * BLOCKS - LAST
    outs = (pltpu.make_async_copy(result.at[pl.ds(0, n_main)], out_refs[0], out_sem.at[0]),
            pltpu.make_async_copy(result.at[pl.ds(n_main, LAST)], out_refs[1], out_sem.at[1]))
    for copy in outs:
        copy.start()
    for piece in range(PIECES):
        for part in range(PARTS):
            for direction in range(2):
                near(piece, part, direction, 0).wait_send()
                hop(piece, part, direction, 0).wait_send()
                forward(piece, part, direction).wait_send()
    for slot in range(n_stage):
        hand_over(0, 0, 0, slot).wait_send()
    for copy in outs:
        copy.wait()


def reduce_grads(hid, wid, n_dev):
    rows, width = wid[0].shape
    bm = width // 6
    bn = 2 * bm
    dma = pltpu.SemaphoreType.DMA
    any_spec = pl.BlockSpec(memory_space=pl.ANY)
    f32, bf16 = jnp.float32, jnp.bfloat16
    n_main = PARTS * BLOCKS - LAST
    n_stage = 2
    outs = pl.pallas_call(
        functools.partial(reduce_kernel, rows, bm, 1.0 / n_dev),
        name="reduce_grads",
        out_shape=[
            jax.ShapeDtypeStruct((n_main, bm // 4, bn), f32),
            jax.ShapeDtypeStruct((LAST, bm // 4, bn), f32),
            jax.ShapeDtypeStruct((PARTS, 2, rows // 2, width), bf16),
            jax.ShapeDtypeStruct((2, PARTS, 2, rows // 2, 4 * bm), bf16),
        ],
        in_specs=[any_spec] * 8,
        out_specs=[any_spec] * 4,
        scratch_shapes=[
            pltpu.VMEM((2, PARTS, RING * rows, 4 * bm), bf16),
            pltpu.VMEM((PARTS, RING * rows, width), bf16),
            pltpu.VMEM((PARTS, CHUNKS, BLOCKS, bm, bn), f32),
            pltpu.VMEM((n_stage, bm, bn), f32),
            pltpu.VMEM((PARTS, 2, RING - 1, BLOCKS, bm // 2, bn), f32),
            pltpu.VMEM((PARTS, 2, RING - 1, BLOCKS, bm // 8, bn), f32),
            pltpu.VMEM((PARTS * BLOCKS, bm // 4, bn), f32),
            dma((PIECES, PARTS)),
            dma((PIECES, PARTS, 2)), dma((PIECES, PARTS, 2)),
            dma((PIECES, PARTS, 2)), dma((PIECES, PARTS, 2)),
            dma((PIECES, PARTS, 2)), dma((PIECES, PARTS, 2)),
            dma((n_stage,)), dma((PARTS, CHUNKS, BLOCKS)),
            dma((PARTS, 2, BLOCKS)), dma((PARTS, 2, RING - 1, BLOCKS)),
            dma((PARTS, 2)), dma((PARTS, 2, RING - 1)),
            dma((2,)),
        ],
        compiler_params=pltpu.CompilerParams(collective_id=0, has_side_effects=True, vmem_limit_bytes=67043328),
        cost_estimate=pl.CostEstimate(flops=16 * rows * 24 * bm * width, bytes_accessed=200_000_000, transcendentals=0),
    )(*hid, *wid)
    return outs[0], outs[1]


def place_kernel(shape, first_block, n_blocks, depth, *refs):
    n_z, n_y, n_xc, bm = shape
    bn = 2 * bm
    n_dev = n_z * n_y * n_xc
    gathered, dsts = refs[0], refs[-7:-3]
    slots, in_sem, out_sem = refs[-3:]
    ahead = depth // 2

    def load(dev):
        slot = lax.rem(dev, depth)
        return pltpu.make_async_copy(gathered.at[dev], slots.at[slot], in_sem.at[slot])

    def drain(dev):
        slot = lax.rem(dev, depth)
        return pltpu.make_async_copy(slots.at[slot], gathered.at[0], out_sem.at[slot])

    def store(dev):
        slot = lax.rem(dev, depth)
        xc, y, z = lax.rem(dev, n_xc), lax.rem(lax.div(dev, n_xc), n_y), lax.div(dev, n_xc * n_y)
        x, core = lax.div(xc, 2), lax.rem(xc, 2)
        for part in sorted({(first_block + k) // BLOCKS for k in range(n_blocks)}):
            owner, chunk, quarter = ((x, y, z), (y, z, x), (z, x, y))[part]
            for which in range(4):
                @pl.when(owner == which)
                def _():
                    for k in range(n_blocks):
                        if (first_block + k) // BLOCKS != part:
                            continue
                        block = (first_block + k) % BLOCKS
                        if which % 2 == 1:
                            row = (8 * part + 4 * core + chunk) * bm + quarter * (bm // 4)
                            col = block * bn
                        else:
                            index = 3 * chunk + block
                            row = lax.div(index, 2) * bm + quarter * (bm // 4)
                            col = (4 * part + 2 * core + lax.rem(index, 2)) * bn
                        row = pl.multiple_of(row, bm // 4)
                        col = pl.multiple_of(col, bn)
                        pltpu.make_async_copy(
                            slots.at[slot, k], dsts[which].at[pl.ds(row, bm // 4), pl.ds(col, bn)], out_sem.at[slot]).start()

    def prime(dev, carry):
        load(dev).start()
        return carry

    def turn(dev, carry):
        @pl.when(dev + ahead < n_dev)
        def _():
            @pl.when(dev + ahead >= depth)
            def _():
                drain(dev + ahead - depth).wait()

            load(dev + ahead).start()

        load(dev).wait()
        store(dev)
        return carry

    def finish(dev, carry):
        drain(dev).wait()
        return carry

    lax.fori_loop(0, ahead, prime, 0)
    lax.fori_loop(0, n_dev, turn, 0)
    lax.fori_loop(n_dev - depth, n_dev, finish, 0)


def place(gathered, first_block, mesh_shape, shapes, earlier=()):
    n_dev, n_blocks, quarter, bn = gathered.shape
    depth = 16
    return pl.pallas_call(
        functools.partial(place_kernel, (*mesh_shape, bn // 2), first_block, n_blocks, depth),
        name="place_grads",
        out_shape=[jax.ShapeDtypeStruct(s, jnp.float32) for s in shapes],
        in_specs=[pl.BlockSpec(memory_space=pl.ANY)] * (1 + len(earlier)),
        out_specs=[pl.BlockSpec(memory_space=pl.ANY)] * 4,
        scratch_shapes=[pltpu.VMEM((depth, n_blocks, quarter, bn), jnp.float32), pltpu.SemaphoreType.DMA((depth,)), pltpu.SemaphoreType.DMA((depth,))],
        input_output_aliases={1 + k: k for k in range(len(earlier))},
        cost_estimate=pl.CostEstimate(flops=8 * gathered.size, bytes_accessed=8 * gathered.size, transcendentals=0),
    )(gathered, *earlier)


def solution(mesh):
    n_dev = math.prod(mesh.shape.values())
    axes = ("z", "y", "xc")
    batch_spec = P(axes, None)
    whole_spec = P(None, None)

    def device_step(x_loc, g_loc, w_one, w_two, w_three, w_four):
        a_one = jnp.dot(x_loc, w_one, preferred_element_type=jnp.float32).astype(jnp.bfloat16)
        h_one = gelu_value(a_one.astype(jnp.float32)).astype(jnp.bfloat16)
        h_two = (jnp.dot(h_one, w_two, preferred_element_type=jnp.float32) + x_loc.astype(jnp.float32)).astype(jnp.bfloat16)
        a_three = jnp.dot(h_two, w_three, preferred_element_type=jnp.float32).astype(jnp.bfloat16)
        h_three = gelu_value(a_three.astype(jnp.float32)).astype(jnp.bfloat16)
        d_a3 = (jnp.einsum("nd,fd->nf", g_loc, w_four, preferred_element_type=jnp.float32) * gelu_grad(a_three.astype(jnp.float32))).astype(jnp.bfloat16)
        d_h2 = (jnp.einsum("nf,df->nd", d_a3, w_three, preferred_element_type=jnp.float32) + g_loc.astype(jnp.float32)).astype(jnp.bfloat16)
        d_a1 = (jnp.einsum("nd,fd->nf", d_h2, w_two, preferred_element_type=jnp.float32) * gelu_grad(a_one.astype(jnp.float32))).astype(jnp.bfloat16)
        main, last = reduce_grads((d_a1, h_one, d_a3, h_three), (x_loc, d_h2, h_two, g_loc), n_dev)
        all_main = lax.all_gather(main, axes, axis=0)
        last, all_main = lax.optimization_barrier((last, all_main))
        all_last = lax.all_gather(last, axes, axis=0)
        shapes = (w_one.shape, w_two.shape, w_three.shape, w_four.shape)
        mesh_shape = tuple(mesh.shape[name] for name in axes)
        grads = place(all_main, 0, mesh_shape, shapes)
        return tuple(place(all_last, PARTS * BLOCKS - LAST, mesh_shape, shapes, grads))

    return jax.shard_map(
        device_step,
        mesh=mesh,
        in_specs=(batch_spec, batch_spec, whole_spec, whole_spec, whole_spec, whole_spec),
        out_specs=(whole_spec, whole_spec, whole_spec, whole_spec),
        check_vma=False,
    )
```

time: 2190 us -> 657 us (0.30)
  waiting for transfers between devices: 1880 us -> 288 us
  Pallas kernels: 0 us -> 284 us
  other arithmetic: 111 us -> 0.01 us
  matrix products: 128 us -> 70.9 us
  local copies, waits for them, and re-layouts: 51.1 us -> 0.05 us
    all_gather x8 -> x2, waiting for transfers between devices: 839 us -> 288 us  [the longest x1 288 us: device_step(): all_main = lax.all_gather(main, axes, axis=0)]
    reduce_scatter x4 -> x0, waiting for transfers between devices: 489 us -> none  [the longest x2 386 us: reduce_grad(): lax.psum_scatter(local_grad, 'xc', scatter_dimension=0, tiled=True)]
    unnamed x21 -> x2, waiting for transfers between devices: 383 us -> 0.03 us
    pallas_call x0 -> x3, Pallas kernels: none -> 284 us  [the longest x1 180 us: reduce_grads(): pl.pallas_call(functools.partial(reduce_kernel, rows, bm, 1.0 / n_dev), n...]
    psum x1 -> x0, waiting for transfers between devices: 168 us -> none  [reduce_grad(): reduced = lax.psum(reduced, 'z')]
    div x4 -> x0, other arithmetic: 111 us -> none  [reduce_grad(): return reduced / n_dev]
    dot_general x3 -> x1, matrix products: 59.1 us -> 12.6 us  [device_step(): jnp.einsum('nd,fd->nf', d_h2, w_two, preferred_element_type=jnp.float32)]
    unnamed x13 -> x20, local copies, waits for them, and re-layouts: 45.9 us -> 0.05 us
  transfers between devices with their start and end apart: 17 -> 2, of which waited for: 17 -> 1; matrix products, arithmetic and copies ran while one was open for 9% -> 0% of each run, Pallas kernels for 0% -> 13%
where the time goes in v2:
time: 657 us; the launch traced here: 656 us
  waiting for transfers between devices  288 us (44%)
  Pallas kernels  284 us (43%)
  matrix products  70.9 us (11%)
  between operations  14.2 us (2%)
    all_gather x1, waiting for transfers between devices, device_step(): all_main = lax.all_gather(main, axes, axis=0)  288 us
    pallas_call x1, Pallas kernels, reduce_grads(): pl.pallas_call(functools.partial(reduce_kernel, rows, bm, 1.0 / n_dev), n...  180 us
    pallas_call x2, Pallas kernels, place(): pl.pallas_call(functools.partial(place_kernel, (*mesh_shape, bn // 2), fi...  104 us
    dot_general x1, matrix products, device_step(): jnp.dot(x_loc, w_one, preferred_element_type=jnp.float32)  14.7 us
  transfers between devices with their start and end apart: 2, of which 1 were waited for; matrix products, arithmetic and copies ran while one was open for 0% of the time, Pallas kernels for 13%

profile of v2, /device:TPU:1, one launch (start us, length us, event | category | flops | bytes accessed | tf_op | source)
XLA Modules:
  0.0 656.4 jit_solution(2845986732173803375)
XLA Ops:
  7.2 0.0 copy-start.1
  7.2 0.0 all-gather.5.cloned.1.call-start
  7.2 0.0 slice-start
  7.2 0.0 slice-start.1
  7.2 0.0 slice-start.2
  7.3 14.7 %fusion.10 = (bf16[256,6144]{1,0:T(8,128)(2,1)}, bf16[256,6144]{1,0:T(8,128)(2,1)}) fusion(bf16[256,1536]{1,0:T(8,128)(2,1)} %refs_4_.1, bf16[1536,6144]{1,0:T(8,128)(2,1)} %param.8), kind=kOutput, calls=%fused_computation.28 | convolution fusion | flops 4849139712 | bytes 25952256 | tf_op jit(solution)/shard_map/dot_general | solution.py:409
  21.9 0.0 copy-done.1
  22.0 13.1 %fusion.20.refs_6_ = bf16[256,1536]{1,0:T(8,128)(2,1)S(1)} fusion(bf16[6144,1536]{1,0:T(8,128)(2,1)} %param.9, bf16[256,1536]{1,0:T(8,128)(2,1)S(1)} %copy-done.1, bf16[256,6144]{1,0:T(8,128)(2,1)} %get-tuple-element.21), kind=kOutput, calls=%fused_computation.40 | convolution fusion | flops 4848746496 | bytes 23592960 | tf_op jit(solution)/shard_map/dot_general | solution.py:411
  35.0 0.0 slice-done
  35.0 0.0 slice-done.1
  35.0 0.0 slice-done.2
  35.1 0.0 slice-done.3
  35.1 0.0 slice-done.4
  35.1 0.0 copy-start.3
  35.1 0.0 copy-start
  35.1 7.8 %fusion.9 = (bf16[256,6144]{1,0:T(8,128)(2,1)}, bf16[256,6144]{1,0:T(8,128)(2,1)S(1)}) fusion(bf16[256,1536]{1,0:T(8,128)(2,1)S(1)} %fusion.20.refs_6_, bf16[1536,6144]{1,0:T(8,128)(2,1)S(1)} %bitcast.15), kind=kOutput, calls=%fused_computation.27 | convolution fusion | flops 4849139712 | bytes 25952256 | tf_op jit(solution)/shard_map/dot_general | solution.py:412
  42.9 0.0 copy-done.3
  42.9 0.0 copy-done
  42.9 12.7 %fusion.refs_2_ = bf16[256,6144]{1,0:T(8,128)(2,1)} fusion(bf16[256,1536]{1,0:T(8,128)(2,1)S(1)} %copy-done, bf16[6144,1536]{1,0:T(8,128)(2,1)} %param.11, bf16[256,6144]{1,0:T(8,128)(2,1)S(1)} %get-tuple-element.23), kind=kOutput, calls=%fused_computation.16 | convolution fusion | flops 4863295488 | bytes 25952256 | tf_op jit(solution)/shard_map/nd,fd->nf/dot_general | solution.py:414
  55.5 10.1 %fusion.21.refs_5_ = bf16[256,1536]{1,0:T(8,128)(2,1)S(1)} fusion(bf16[256,6144]{1,0:T(8,128)(2,1)} %fusion.refs_2_, bf16[1536,6144]{1,0:T(8,128)(2,1)} %param.10, bf16[256,1536]{1,0:T(8,128)(2,1)S(1)} %copy-done), kind=kOutput, calls=%fused_computation.41 | convolution fusion | flops 4833017856 | bytes 23592960 | tf_op jit(solution)/shard_map/nf,df->nd/dot_general | solution.py:415
  65.6 0.0 copy-done.2
  65.6 0.0 copy-start.4
  65.6 12.6 %fusion.1.refs_0_ = bf16[256,6144]{1,0:T(8,128)(2,1)} fusion(bf16[256,1536]{1,0:T(8,128)(2,1)S(1)} %fusion.21.refs_5_, bf16[6144,1536]{1,0:T(8,128)(2,1)} %param.9, bf16[256,6144]{1,0:T(8,128)(2,1)S(1)} %copy-done.2), kind=kOutput, calls=%fused_computation.17 | convolution fusion | flops 4863295488 | bytes 25952256 | tf_op jit(solution)/shard_map/nd,fd->nf/dot_general | solution.py:416
  78.3 0.0 copy-done.4
  78.3 179.9 %reduce_grads.1 = (f32[8,64,512]{2,1,0:T(8,128)}, f32[1,64,512]{2,1,0:T(8,128)}, bf16[3,2,128,1536]{3,2,1,0:T(8,128)(2,1)}, bf16[2,3,2,128,1024]{4,3,2,1,0:T(8,128)(2,1)}) custom-call(bf16[256,6144]{1,0:T(8,128)(2,1)} %fusion.1.refs_0_, bf16[256,6144]{1,0:T(8,128)(2,1)} %get-tuple-element.20.refs_1_, bf16[256,6144]{1,0:T(8,128)(2,1)} %fusion.refs_2_, ...), custom_call_target="tpu_custom_call" | custom-call | flops 38654705664 | bytes 200000000 | tf_op jit(solution)/shard_map/reduce_grads/pallas_call | solution.py:286
  258.2 0.0 all-gather.5.cloned.1.call-update
  258.2 0.0 all-gather.7.cloned.1.call-start
  258.2 287.6 %all-gather.5.cloned.1.call-done = f32[1024,64,512]{2,1,0:T(8,128)} async-done(((f32[8,64,512]{2,1,0:T(8,128)}), f32[1024,64,512]{2,1,0:T(8,128)}) %all-gather.5.cloned.1.call-update) | async-done | bytes 134217744 | tf_op jit(solution)/shard_map/all_gather | solution.py:418
  545.8 0.0 all-gather.7.cloned.1.call-update
  545.8 87.2 %place_grads.2 = (f32[1536,6144]{1,0:T(8,128)}, f32[6144,1536]{1,0:T(8,128)}, f32[1536,6144]{1,0:T(8,128)}, f32[6144,1536]{1,0:T(8,128)}) custom-call(f32[128,8,64,512]{3,2,1,0:T(8,128)} %bitcast.refs_0_), custom_call_target="tpu_custom_call" | custom-call | flops 268435456 | bytes 268435456 | tf_op jit(solution)/shard_map/place_grads/pallas_call | solution.py:390
  633.0 0.0 all-gather.7.cloned.1.call-done
  633.1 16.5 %place_grads.3 = (f32[1536,6144]{1,0:T(8,128)}, f32[6144,1536]{1,0:T(8,128)}, f32[1536,6144]{1,0:T(8,128)}, f32[6144,1536]{1,0:T(8,128)}) custom-call(f32[128,1,64,512]{3,2,1,0:T(8,128)} %bitcast.13, f32[1536,6144]{1,0:T(8,128)} %get-tuple-element.16.refs_1_, ...), custom_call_target="tpu_custom_call", output_to_operand_aliasing={{0}: (1, {}), {1}: (2, {}), {2}: (3, {}), {3}: (4, {})} | custom-call | flops 33554432 | bytes 33554432 | tf_op jit(solution)/shard_map/place_grads/pallas_call | solution.py:390
  (4 shorter events, 0.0 us)
Async XLA Ops:
  7.2 14.8 %copy-start.1 = (bf16[256,1536]{1,0:T(8,128)(2,1)S(1)}, bf16[256,1536]{1,0:T(8,128)(2,1)}, u32[]{:S(2)}) copy-start(bf16[256,1536]{1,0:T(8,128)(2,1)} %refs_4_.1) | copy-start | bytes 2359300
  7.2 538.6 %all-gather.5.cloned.1.call-start = ((), (), s32[]{:S(2)}) async-start(), calls=%async_computation | async-start | bytes 135266304 | tf_op jit(solution)/shard_map/all_gather | solution.py:418
  7.2 27.8 %slice-start = ((s8[18874368]{0:T(1024)(128)(4,1)}), s8[4194304]{0:T(1024)(128)(4,1)S(1)}, s32[]{:S(2)}) async-start(s8[18874368]{0:T(1024)(128)(4,1)} %bitcast.14), calls=%async_computation.2 | async-start | bytes 8388608
  7.2 27.8 %slice-start.1 = ((s8[18874368]{0:T(1024)(128)(4,1)}), s8[4194304]{0:T(1024)(128)(4,1)S(1)}, s32[]{:S(2)}) async-start(s8[18874368]{0:T(1024)(128)(4,1)} %bitcast.14), calls=%async_computation.3 | async-start | bytes 8388608
  7.2 27.8 %slice-start.2 = ((s8[18874368]{0:T(1024)(128)(4,1)}), s8[4194304]{0:T(1024)(128)(4,1)S(1)}, s32[]{:S(2)}) async-start(s8[18874368]{0:T(1024)(128)(4,1)} %bitcast.14), calls=%async_computation.4 | async-start | bytes 8388608
  21.9 13.1 %slice-start.3 = ((s8[18874368]{0:T(1024)(128)(4,1)}), s8[4194304]{0:T(1024)(128)(4,1)S(1)}, s32[]{:S(2)}) async-start(s8[18874368]{0:T(1024)(128)(4,1)} %bitcast.14), calls=%async_computation.5 | async-start | bytes 8388608
  21.9 13.1 %slice-start.4 = ((s8[18874368]{0:T(1024)(128)(4,1)}), s8[2097152]{0:T(1024)(128)(4,1)S(1)}, s32[]{:S(2)}) async-start(s8[18874368]{0:T(1024)(128)(4,1)} %bitcast.14), calls=%async_computation.6 | async-start | bytes 4194304
  35.1 7.8 %copy-start.3 = (bf16[256,1536]{1,0:T(8,128)(2,1)}, bf16[256,1536]{1,0:T(8,128)(2,1)S(1)}, u32[]{:S(2)}) copy-start(bf16[256,1536]{1,0:T(8,128)(2,1)S(1)} %fusion.20.refs_6_) | copy-start | bytes 2359300
  35.1 7.8 %copy-start = (bf16[256,1536]{1,0:T(8,128)(2,1)S(1)}, bf16[256,1536]{1,0:T(8,128)(2,1)}, u32[]{:S(2)}) copy-start(bf16[256,1536]{1,0:T(8,128)(2,1)} %refs_7_.1) | copy-start | bytes 2359300
  55.5 10.1 %copy-start.2 = (bf16[256,6144]{1,0:T(8,128)(2,1)S(1)}, bf16[256,6144]{1,0:T(8,128)(2,1)}, u32[]{:S(2)}) copy-start(bf16[256,6144]{1,0:T(8,128)(2,1)} %get-tuple-element.21) | copy-start | bytes 9437188
  65.6 12.6 %copy-start.4 = (bf16[256,1536]{1,0:T(8,128)(2,1)}, bf16[256,1536]{1,0:T(8,128)(2,1)S(1)}, u32[]{:S(2)}) copy-start(bf16[256,1536]{1,0:T(8,128)(2,1)S(1)} %fusion.21.refs_5_) | copy-start | bytes 2359300
  258.2 374.9 %all-gather.7.cloned.1.call-start = ((), (), s32[]{:S(2)}) async-start(), calls=%async_computation.1 | async-start | bytes 16908288 | tf_op jit(solution)/shard_map/all_gather | solution.py:420
Sparse Core Ops, SparseCore 0:
  258.3 287.4 all-gather.4
  548.9 78.5 all-gather.6
